TPU v7x, 32 devices: a whole 2x2x4 slice. The times are simulated.
32 devices in a mesh: groups: 2 (over y), gx: 4 (over z), gy: 4 (over x, core).
Axes of the slice: x: 2, y: 2, z: 4, core: 2. Of those that a mesh axis runs over, the one named last changes fastest.
Arguments:
- tokens: bfloat16 [2, 16, 16384], P(None, 'groups', 'gx'), parts along dimension 1, may hold values from -20 to 20, as said below
- lengths: int32 [2, 16], P(None, ('groups', 'gx')), parts along dimension 1, may hold values from 1 to 1024, as said below
- norm_gain: bfloat16 [16384], P('gx'), may hold values from 0.5 to 2
- w_query: bfloat16 [16384, 8192], P('gx', 'gy'), may hold values from -1.171875 to 1.171875
- key_value_weight: bfloat16 [16384, 4, 256], P('gx', 'gy'), may hold values from -0.046875 to 0.046875
- w_out: bfloat16 [8192, 16384], P('gy', 'gx'), may hold values from -0.0625 to 0.0625
- cache: bfloat16 [2, 16, 1024, 4, 2, 128], P(None, ('groups', 'gx'), None, 'gy'), parts along dimension 1, may hold values from -16 to 16
Outputs:
- layer_out: bfloat16 [2, 16, 16384], P(None, 'groups', 'gx'), parts along dimension 1
There are 2 independent parts, one for each index of `groups`. A program takes and returns all parts, laid end to end along the dimension named above; an argument that names none is the same for every part. Nothing has to cross between parts.
Inputs may be any that keep to these rules, and one draw needn't show every extreme that they name: `tokens`: entries vary with the feature and the row. `lengths`: some rollout has exactly 1024 cached positions in every draw.
All inputs are finite; a program needn't handle non-finite values.
Results may differ from a plain program's by a relative error of at most 0.012.
The roundings to bfloat16 on the way count: a program that leaves them out, or rounds other values in their place, can miss the bound.
Values may be sent and summed in bfloat16 or wider, within the bound.
A program may use at most 128 MiB of HBM per device.

v0:
```python
import functools

import jax
import jax.numpy as jnp
import numpy as np
from jax import lax
from jax.experimental import pallas as pl
from jax.experimental.pallas import tpu as pltpu
from jax.sharding import PartitionSpec as P

MODEL_WIDTH = 16384
HEAD_SIZE = 128
ROPE_BASE = 500000.0
MESH = pl.DeviceIdType.MESH


def kernel(
    n, ny, q_chunk, o_chunk,
    lens, tok_hbm, gain_hbm, freq_hbm, wq_hbm, wk_hbm, wo_hbm, kv_hbm,
    out,
    tok, gain, freq, wq, wk, wo, kv, normed,
    send, recv, q_s, o_s, att_send, att_recv, x_s, ybuf, r1, s2, r2,
    small_sem, wq_sem, wk_sem, wo_sem, kv_sem,
    qs_sem, qr_sem, as_sem, ar_sem, e_send, e_recv,
):
    batches, rows, depth = tok.shape
    here = rows // n
    total_rows = batches * rows
    q_width = wq.shape[1]
    kv_width = wk.shape[1]
    heads = q_width // HEAD_SIZE
    out_width = wo.shape[1]
    nq = q_width // q_chunk
    no = out_width // o_chunk
    local_rows = batches * here
    positions = kv.shape[0] // local_rows
    me = lax.axis_index("gx")
    my = lax.axis_index("gy")

    smalls = [
        pltpu.make_async_copy(tok_hbm, tok, small_sem.at[0]),
        pltpu.make_async_copy(gain_hbm, gain, small_sem.at[1]),
        pltpu.make_async_copy(freq_hbm, freq, small_sem.at[2]),
    ]
    for copy in smalls:
        copy.start()
    wk_copy = pltpu.make_async_copy(wk_hbm, wk, wk_sem)
    wk_copy.start()

    def wq_copy(c):
        cols = pl.ds(pl.multiple_of(c * q_chunk, q_chunk), q_chunk)
        return pltpu.make_async_copy(wq_hbm.at[:, cols], wq.at[:, cols], wq_sem.at[c])

    def wo_copy(c):
        cols = pl.ds(pl.multiple_of(c * o_chunk, o_chunk), o_chunk)
        return pltpu.make_async_copy(wo_hbm.at[:, cols], wo.at[:, cols], wo_sem.at[c])

    kv_copy = pltpu.make_async_copy(kv_hbm, kv, kv_sem)
    for c in range(nq):
        wq_copy(c).start()

    barrier = pltpu.get_barrier_semaphore()

    def greet(d, carry):
        pl.semaphore_signal(
            barrier, inc=1, device_id={"gx": lax.rem(me + d, n)}, device_id_type=MESH
        )
        return carry

    lax.fori_loop(1, n, greet, 0)
    bits = ny.bit_length() - 1

    def across(level):
        step = 1 << level
        return my + step - 2 * step * lax.rem(my // step, 2)

    for level in range(bits):
        pl.semaphore_signal(barrier, inc=1, device_id={"gy": across(level)}, device_id_type=MESH)

    for copy in smalls:
        copy.wait()
    x = tok[...].astype(jnp.float32).reshape(total_rows, depth)
    for k in range(depth // HEAD_SIZE):
        cols = slice(k * HEAD_SIZE, (k + 1) * HEAD_SIZE)
        normed[:, cols] = (x[:, cols] * gain[k:k + 1, :].astype(jnp.float32)).astype(jnp.bfloat16)
    squares = jnp.broadcast_to(jnp.sum(x * x, axis=1, keepdims=True), (total_rows, HEAD_SIZE))

    def put(part, start):
        width = part.shape[1]
        for j in range(n):
            for b in range(batches):
                send[j, b * here:(b + 1) * here, pl.ds(start, width)] = part[
                    b * rows + j * here:b * rows + (j + 1) * here, :
                ]

    def shift(c, d, start, width):
        target = lax.rem(me + d, n)
        cols = pl.ds(start, width)
        return pltpu.make_async_remote_copy(
            src_ref=send.at[target, :, cols],
            dst_ref=recv.at[me, :, cols],
            send_sem=qs_sem.at[c, d],
            recv_sem=qr_sem.at[c, d],
            device_id={"gx": target},
            device_id_type=MESH,
        )

    def arrive(c, d, start, width):
        source = lax.rem(me - d + n, n)
        cols = pl.ds(start, width)
        return pltpu.make_async_remote_copy(
            src_ref=send.at[source, :, cols],
            dst_ref=recv.at[source, :, cols],
            send_sem=qs_sem.at[c, d],
            recv_sem=qr_sem.at[c, d],
            device_id={"gx": source},
            device_id_type=MESH,
        )

    def each(fn):
        def body(d, carry):
            fn(d)
            return carry
        lax.fori_loop(1, n, body, 0)

    wk_copy.wait()
    xn = normed[...]
    put(jnp.dot(xn, wk[...], preferred_element_type=jnp.float32), q_width)
    put(squares, q_width + kv_width)
    pl.semaphore_wait(barrier, n - 1 + bits)
    side = kv_width + HEAD_SIZE
    each(lambda d: shift(nq, d, q_width, side).start())

    def project(c, carry):
        start = pl.multiple_of(c * q_chunk, q_chunk)
        wq_copy(c).wait()

        @pl.when(c == max(nq - 2, 0))
        def _():
            kv_copy.start()
            for o in range(no):
                wo_copy(o).start()

        put(
            jnp.dot(
                normed[...], wq[:, pl.ds(start, q_chunk)], preferred_element_type=jnp.float32
            ),
            start,
        )
        each(lambda d: shift(c, d, start, q_chunk).start())
        return carry

    lax.fori_loop(0, nq, project, 0)

    lane = lax.broadcasted_iota(jnp.int32, (local_rows, HEAD_SIZE), 1)
    row = lax.broadcasted_iota(jnp.int32, (local_rows, HEAD_SIZE), 0)
    place = jnp.zeros((local_rows, HEAD_SIZE), jnp.float32)
    for r in range(local_rows):
        place = jnp.where(row == r, lens[r // here, r % here].astype(jnp.float32), place)
    angle = place * freq[...]
    cosine = jnp.cos(angle)
    sine = jnp.sin(angle)
    sine = jnp.where(lane < HEAD_SIZE // 2, -sine, sine)

    def rotate(v):
        return v * cosine + pltpu.roll(v, HEAD_SIZE // 2, 1) * sine

    def finish(c, start, width):
        each(lambda d: arrive(c, d, start, width).wait_recv())

    def summed(start, width):
        cols = pl.ds(start, width)
        total = send[me, :, cols]

        def add(d, acc):
            return acc + recv[lax.rem(me + d, n), :, cols]

        return lax.fori_loop(1, n, add, total, unroll=n <= 8)

    finish(nq, q_width, side)
    tail = summed(q_width, side)
    scale = lax.rsqrt(tail[:, kv_width:] / MODEL_WIDTH + 1e-05)
    rkey = rotate(tail[:, :HEAD_SIZE] * scale)
    value_new = tail[:, HEAD_SIZE:2 * HEAD_SIZE] * scale

    for c in range(nq):
        finish(c, c * q_chunk, q_chunk)
        block = summed(c * q_chunk, q_chunk)
        for h in range(q_chunk // HEAD_SIZE):
            q_s[:, c * (q_chunk // HEAD_SIZE) + h, :] = rotate(
                block[:, h * HEAD_SIZE:(h + 1) * HEAD_SIZE] * scale
            )

    kv_copy.wait()
    inv_root = np.float32(1.0 / np.sqrt(np.float32(HEAD_SIZE)))
    column = lax.broadcasted_iota(jnp.int32, (heads, positions), 1)
    is_key = lax.rem(column, 2) == 0
    for r in range(local_rows):
        pairs = kv[r * positions:(r + 1) * positions, :]
        rquery = q_s[r].astype(jnp.bfloat16)
        scores = (
            lax.dot_general(
                rquery, pairs, (((1,), (1,)), ((), ())), preferred_element_type=jnp.float32
            )
            * inv_root
        )
        valid = jnp.logical_and(is_key, column < 2 * lens[r // here, r % here])
        scores = jnp.where(valid, scores, -1e30)
        new_score = (
            jnp.sum(rquery.astype(jnp.float32) * rkey[r:r + 1, :], axis=1, keepdims=True)
            * inv_root
        )
        top = jnp.maximum(jnp.max(scores, axis=1, keepdims=True), new_score)
        weights = jnp.exp(scores - top)
        new_weight = jnp.exp(new_score - top)
        total = jnp.sum(weights, axis=1, keepdims=True) + new_weight
        moved = pltpu.roll(weights, 1, 1).astype(jnp.bfloat16)
        mixed = jnp.dot(moved, pairs, preferred_element_type=jnp.float32)
        o_s[r] = (mixed + new_weight * value_new[r:r + 1, :]) / total

    for h in range(heads):
        att_send[:, h * HEAD_SIZE:(h + 1) * HEAD_SIZE] = o_s[:, h, :].astype(jnp.bfloat16)

    def spread(d):
        target = lax.rem(me + d, n)
        return pltpu.make_async_remote_copy(
            src_ref=att_send, dst_ref=att_recv.at[me],
            send_sem=as_sem.at[d], recv_sem=ar_sem.at[d],
            device_id={"gx": target}, device_id_type=MESH,
        )

    def gathered(d):
        source = lax.rem(me - d + n, n)
        return pltpu.make_async_remote_copy(
            src_ref=att_send, dst_ref=att_recv.at[source],
            send_sem=as_sem.at[d], recv_sem=ar_sem.at[d],
            device_id={"gx": source}, device_id_type=MESH,
        )

    each(lambda d: spread(d).start())
    att_recv[me] = att_send[...]
    each(lambda d: gathered(d).wait_recv())
    for j in range(n):
        block = att_recv[j].astype(jnp.float32)
        for b in range(batches):
            x_s[b * rows + j * here:b * rows + (j + 1) * here, :] = block[
                b * here:(b + 1) * here, :
            ]
    normed_att = x_s[...].astype(jnp.bfloat16)

    def cols_of(c):
        return pl.ds(pl.multiple_of(c * o_chunk, o_chunk), o_chunk)

    def exchange(c, k):
        cols = cols_of(c)
        return pltpu.make_async_remote_copy(
            src_ref=ybuf.at[:, cols] if k == 0 else s2.at[k - 1, :, cols],
            dst_ref=r1.at[:, cols] if k == 0 else r2.at[k - 1, :, cols],
            send_sem=e_send.at[k, c], recv_sem=e_recv.at[k, c],
            device_id={"gy": across(bits - 1 - k)}, device_id_type=MESH,
        )

    def multiply(c):
        cols = cols_of(c)
        wo_copy(c).wait()
        ybuf[:, cols] = jnp.dot(
            normed_att, wo[:, cols], preferred_element_type=jnp.float32
        ).astype(jnp.bfloat16)
        exchange(c, 0).start()

    def so_far(c, k):
        cols = cols_of(c)
        exchange(c, k).wait_recv()
        if k == 0:
            return ybuf[:, cols].astype(jnp.float32) + r1[:, cols].astype(jnp.float32)
        return s2[k - 1, :, cols] + r2[k - 1, :, cols]

    def combine(c, k):
        s2[k, :, cols_of(c)] = so_far(c, k)
        exchange(c, k + 1).start()

    def close(c):
        cols = cols_of(c)
        total = so_far(c, bits - 1).reshape(batches, rows, o_chunk)
        out[:, :, cols] = (tok[:, :, cols].astype(jnp.float32) + total).astype(jnp.bfloat16)

    stages = [(0, multiply)]
    for k in range(bits - 1):
        stages.append((stages[-1][0] + 3, functools.partial(combine, k=k)))
    stages.append((stages[-1][0] + 1, close))

    def tick(t, carry):
        for lag, stage in stages:
            @pl.when(jnp.logical_and(t >= lag, t < no + lag))
            def _(lag=lag, stage=stage):
                stage(t - lag)
        return carry

    lax.fori_loop(0, no + stages[-1][0], tick, 0)

    def drain(c, carry):
        for k in range(bits):
            exchange(c, k).wait_send()
        return carry

    lax.fori_loop(0, no, drain, 0)
    each(lambda d: spread(d).wait_send())
    each(lambda d: shift(nq, d, q_width, side).wait_send())
    for c in range(nq):
        each(lambda d: shift(c, d, c * q_chunk, q_chunk).wait_send())


def local(n, ny, tokens, lengths, norm_gain, w_query, key_value_weight, w_out, cache):
    batches, rows, depth = tokens.shape
    here = rows // n
    local_rows = batches * here
    q_width = w_query.shape[1]
    kv_heads = key_value_weight.shape[1]
    kv_width = kv_heads * key_value_weight.shape[2]
    assert kv_heads == 1 and ny >= 4 and ny & (ny - 1) == 0
    heads = q_width // HEAD_SIZE
    out_width = w_out.shape[1]
    q_chunk = 1024 if n <= 8 else q_width
    o_chunk = min(1024, out_width)
    nq, no = q_width // q_chunk, out_width // o_chunk
    bits = ny.bit_length() - 1
    wide = q_width + kv_width + HEAD_SIZE
    freq = np.float32(ROPE_BASE) ** (
        -2.0 * np.arange(HEAD_SIZE // 2, dtype=np.float32) / HEAD_SIZE
    )
    freq = np.concatenate([freq, freq]).astype(np.float32)[None, :]
    pairs = cache.reshape(local_rows * cache.shape[2] * 2, HEAD_SIZE)
    any_space = pl.BlockSpec(memory_space=pltpu.HBM)
    f32, bf16 = jnp.float32, jnp.bfloat16
    dma = pltpu.SemaphoreType.DMA
    return pl.pallas_call(
        functools.partial(kernel, n, ny, q_chunk, o_chunk),
        out_shape=pltpu.VMEM(tokens.shape, bf16),
        in_specs=[pl.BlockSpec(memory_space=pltpu.SMEM)] + [any_space] * 7,
        out_specs=pl.BlockSpec(memory_space=pltpu.VMEM),
        scratch_shapes=[
            pltpu.VMEM(tokens.shape, bf16),
            pltpu.VMEM((depth // HEAD_SIZE, HEAD_SIZE), bf16),
            pltpu.VMEM((1, HEAD_SIZE), f32),
            pltpu.VMEM(w_query.shape, bf16),
            pltpu.VMEM((depth, kv_width), bf16),
            pltpu.VMEM(w_out.shape, bf16),
            pltpu.VMEM(pairs.shape, bf16),
            pltpu.VMEM((batches * rows, depth), bf16),
            pltpu.VMEM((n, local_rows, wide), f32),
            pltpu.VMEM((n, local_rows, wide), f32),
            pltpu.VMEM((local_rows, heads, HEAD_SIZE), f32),
            pltpu.VMEM((local_rows, heads, HEAD_SIZE), f32),
            pltpu.VMEM((local_rows, q_width), bf16),
            pltpu.VMEM((n, local_rows, q_width), bf16),
            pltpu.VMEM((batches * rows, q_width), f32),
            pltpu.VMEM((batches * rows, out_width), bf16),
            pltpu.VMEM((batches * rows, out_width), bf16),
            pltpu.VMEM((bits - 1, batches * rows, out_width), f32),
            pltpu.VMEM((bits - 1, batches * rows, out_width), f32),
            dma((3,)), dma((nq,)), dma, dma((no,)), dma,
            dma((nq + 1, n)), dma((nq + 1, n)), dma((n,)), dma((n,)),
            dma((bits, no)), dma((bits, no)),
        ],
        compiler_params=pltpu.CompilerParams(
            collective_id=0, has_side_effects=True, vmem_limit_bytes=67043328 - 2 * tokens.size
        ),
    )(
        lengths, tokens, norm_gain.reshape(depth // HEAD_SIZE, HEAD_SIZE), jnp.asarray(freq),
        w_query, key_value_weight.reshape(depth, kv_width), w_out, pairs,
    )


def solution(mesh):
    placed = (
        P(None, "groups", "gx"),
        P(None, ("groups", "gx")),
        P("gx"),
        P("gx", "gy"),
        P("gx", "gy", None),
        P("gy", "gx"),
        P(None, ("groups", "gx"), None, "gy", None, None),
    )
    return jax.shard_map(
        functools.partial(local, mesh.shape["gx"], mesh.shape["gy"]),
        mesh=mesh, in_specs=placed, out_specs=P(None, "groups", "gx"), check_vma=False,
    )
```

profile of v0, /device:TPU:0, one launch (start us, length us, event | category | flops | bytes accessed | tf_op | source)
XLA Modules:
  0.0 28.4 jit_solution(1996853774373217445)
XLA Ops:
  0.0 27.7 %shard_map.82 = bf16[2,8,4096]{2,1,0:T(8,128)(2,1)S(1)} custom-call(s32[2,2]{1,0:T(2,128)} %lens.1, bf16[2,8,4096]{2,1,0:T(8,128)(2,1)} %tok_hbm.1, bf16[32,128]{1,0:T(8,128)(2,1)} %bitcast.5, f32[1,128]{1,0:T(1,128)} %constant.2.clone.freq_hbm, bf16[4096,2048]{1,0:T(8,128)(2,1)} %wq_hbm.1, bf16[4096,256]{1,0:T(8,128)(2,1)} %bitcast.3, ...), custom_call_target="tpu_custom_call" | custom-call | tf_op jit(solution)/shard_map/pallas_call | solution.py:336
  27.7 0.7 %copy.10 = bf16[2,8,4096]{2,1,0:T(8,128)(2,1)} copy(bf16[2,8,4096]{2,1,0:T(8,128)(2,1)S(1)} %shard_map.82) | data formatting | bytes 262144
where the time goes:
time: 28.5 us; the launch traced here: 28.4 us
  Pallas kernels  27.7 us (97%)
  local copies, waits for them, and re-layouts  0.66 us (2%)
    pallas_call x1, Pallas kernels, local(): pl.pallas_call(functools.partial(kernel, n, ny, q_chunk, o_chunk), out_sh...  27.7 us
    unnamed x1, local copies, waits for them, and re-layouts  0.66 us

commit v1 on v0

v1 whole, which is shorter than its diff:
```python
import functools

import jax
import jax.numpy as jnp
import numpy as np
from jax import lax
from jax.experimental import pallas as pl
from jax.experimental.pallas import tpu as pltpu
from jax.sharding import PartitionSpec as P

MODEL_WIDTH = 16384
HEAD_SIZE = 128
ROPE_BASE = 500000.0
MESH = pl.DeviceIdType.MESH


def kernel(
    n, ny, hc, splits, o_chunk,
    lens_hbm, tok_hbm, gain_hbm, freq_hbm, wq_hbm, wk_hbm, wo_hbm, kv_hbm,
    out,
    lens, tok, gain, freq, wq, wk, wo, kv, normed,
    send, recv, tail_send, tail_recv, att_send, att_recv, x_f, x_s,
    ybuf, fold_s, fold_r, cross_s, cross_r,
    small_sem, wq_sem, wk_sem, wo_sem, kv_sem,
    qs_sem, qr_sem, as_sem, ar_sem, fs_sem, fr_sem, cs_sem, cr_sem, os_sem, or_sem,
):
    batches, rows, depth = tok.shape
    here = rows // n
    total_rows = batches * rows
    q_width = wq.shape[1]
    kv_width = wk.shape[1]
    heads = q_width // HEAD_SIZE
    out_width = wo.shape[1]
    nq = heads // hc
    no = out_width // o_chunk
    local_rows = batches * here
    pairs = local_rows // 2
    positions = kv.shape[1]
    q_chunk = hc * HEAD_SIZE
    k_part = depth // splits
    bits = ny.bit_length() - 1
    me = lax.axis_index("gx")
    my = lax.axis_index("gy")
    leader = lax.rem(my, 2) == 1
    follower = lax.rem(my, 2) == 0

    smalls = [
        pltpu.make_async_copy(tok_hbm, tok, small_sem.at[0]),
        pltpu.make_async_copy(gain_hbm, gain, small_sem.at[1]),
        pltpu.make_async_copy(freq_hbm, freq, small_sem.at[2]),
        pltpu.make_async_copy(lens_hbm, lens, small_sem.at[3]),
    ]

    def wq_copy(c, k):
        at = (pl.ds(k * k_part, k_part), pl.ds(c * q_chunk, q_chunk))
        return pltpu.make_async_copy(wq_hbm.at[at], wq.at[at], wq_sem.at[c, k])

    def wo_copy(c):
        at = pl.ds(c * q_chunk, q_chunk)
        return pltpu.make_async_copy(wo_hbm.at[at], wo.at[at], wo_sem.at[c])

    def kv_copy(r):
        return pltpu.make_async_copy(
            kv_hbm.at[pl.ds(r * positions, positions)],
            kv.at[r // 2, :, pl.ds((r % 2) * HEAD_SIZE, HEAD_SIZE)],
            kv_sem.at[r],
        )

    for copy in smalls:
        copy.start()
    wk_copy = pltpu.make_async_copy(wk_hbm, wk, wk_sem)
    wk_copy.start()
    for c in range(nq):
        for k in range(splits):
            wq_copy(c, k).start()
    for r in range(local_rows):
        kv_copy(r).start()
    for c in range(nq):
        wo_copy(c).start()

    barrier = pltpu.get_barrier_semaphore()

    def each(fn):
        if n <= 8:
            for d in range(1, n):
                fn(d)
        else:
            def body(d, carry):
                fn(d)
                return carry
            lax.fori_loop(1, n, body, 0)

    def greet(d):
        pl.semaphore_signal(
            barrier, inc=1, device_id={"gx": lax.rem(me + d, n)}, device_id_type=MESH
        )

    each(greet)

    def across(level):
        step = 1 << level
        return my + step - 2 * step * lax.rem(my // step, 2)

    for level in range(bits):
        pl.semaphore_signal(barrier, inc=1, device_id={"gy": across(level)}, device_id_type=MESH)

    for copy in smalls:
        copy.wait()
    x = tok[...].astype(jnp.float32).reshape(total_rows, depth)
    for k in range(depth // HEAD_SIZE):
        cols = slice(k * HEAD_SIZE, (k + 1) * HEAD_SIZE)
        normed[:, cols] = (x[:, cols] * gain[k:k + 1, :].astype(jnp.float32)).astype(jnp.bfloat16)
    squares = jnp.broadcast_to(jnp.sum(x * x, axis=1, keepdims=True), (total_rows, HEAD_SIZE))

    def to(d):
        return lax.rem(me + d, n)

    def source(d):
        return lax.rem(me - d + n, n)

    def shift(c, d, peer):
        src, dst = (tail_send, tail_recv) if c == nq else (send.at[c], recv.at[c])
        return pltpu.make_async_remote_copy(
            src_ref=src.at[to(d)],
            dst_ref=dst.at[peer],
            send_sem=qs_sem.at[c, d],
            recv_sem=qr_sem.at[c, d],
            device_id={"gx": to(d)},
            device_id_type=MESH,
        )

    wk_copy.wait()
    keyval = jnp.dot(normed[...], wk[...], preferred_element_type=jnp.float32)
    for j in range(n):
        for b in range(batches):
            at = slice(b * rows + j * here, b * rows + (j + 1) * here)
            to_at = slice(b * here, (b + 1) * here)
            tail_send[j, to_at, :kv_width] = keyval[at]
            tail_send[j, to_at, kv_width:] = squares[at]
    pl.semaphore_wait(barrier, n - 1 + bits)
    each(lambda d: shift(nq, d, me).start())

    group = local_rows * hc
    for c in range(nq):
        part = None
        for k in range(splits):
            wq_copy(c, k).wait()
            ks = slice(k * k_part, (k + 1) * k_part)
            piece = jnp.dot(
                normed[:, ks], wq[ks, c * q_chunk:(c + 1) * q_chunk],
                preferred_element_type=jnp.float32,
            )
            part = piece if part is None else part + piece
        for j in range(n):
            for b in range(batches):
                at = slice(b * rows + j * here, b * rows + (j + 1) * here)
                for h in range(hc):
                    send[c, j, pl.ds(b * here * hc + h, here, stride=hc), :] = part[
                        at, h * HEAD_SIZE:(h + 1) * HEAD_SIZE
                    ]
        each(lambda d: shift(c, d, me).start())

    lane = lax.broadcasted_iota(jnp.int32, (group, HEAD_SIZE), 1)
    owner = lax.broadcasted_iota(jnp.int32, (group, HEAD_SIZE), 0) // hc
    place = jnp.zeros((group, HEAD_SIZE), jnp.float32)
    for r in range(local_rows):
        place = jnp.where(owner == r, lens[r // here, r % here].astype(jnp.float32), place)
    angle = place * freq[...]
    cosine = jnp.cos(angle)
    sine = jnp.sin(angle)
    sine = jnp.where(lane < HEAD_SIZE // 2, -sine, sine)

    def rotate(v):
        return v * cosine + pltpu.roll(v, HEAD_SIZE // 2, 1) * sine

    def wait_from(c):
        each(lambda d: shift(c, d, source(d)).wait_recv())

    def summed(mine, theirs):
        def add(d, acc):
            return acc + theirs[to(d)]
        return lax.fori_loop(1, n, add, mine[me], unroll=n <= 8)

    wait_from(nq)
    tail = summed(tail_send, tail_recv)

    def spread_rows(v):
        return jnp.concatenate(
            [jnp.broadcast_to(v[r:r + 1], (hc, v.shape[1])) for r in range(local_rows)], axis=0
        )

    scale = lax.rsqrt(spread_rows(tail[:, kv_width:]) / MODEL_WIDTH + 1e-05)
    rkey = rotate(spread_rows(tail[:, :HEAD_SIZE]) * scale)
    value_new = spread_rows(tail[:, HEAD_SIZE:2 * HEAD_SIZE]) * scale

    inv_root = np.float32(1.0 / np.sqrt(np.float32(HEAD_SIZE)))
    column = lax.broadcasted_iota(jnp.int32, (2 * hc, positions), 1)
    key_column = jnp.where(lax.rem(column, 2) == 0, column, 2 * positions)
    first = lax.broadcasted_iota(jnp.int32, (2 * hc, HEAD_SIZE), 0) < hc
    first_wide = lax.broadcasted_iota(jnp.int32, (2 * hc, positions), 0) < hc

    def spread(c, d, peer):
        return pltpu.make_async_remote_copy(
            src_ref=att_send.at[c], dst_ref=att_recv.at[c, peer],
            send_sem=as_sem.at[c, d], recv_sem=ar_sem.at[c, d],
            device_id={"gx": to(d)}, device_id_type=MESH,
        )

    for c in range(nq):
        wait_from(c)
        rquery = rotate(summed(send.at[c], recv.at[c]) * scale).astype(jnp.bfloat16)
        rquery = rquery.astype(jnp.float32)
        new_scores = jnp.sum(rquery * rkey, axis=1, keepdims=True) * inv_root
        done = []
        for p in range(pairs):
            if c == 0:
                kv_copy(2 * p).wait()
                kv_copy(2 * p + 1).wait()
            at = slice(p * 2 * hc, (p + 1) * 2 * hc)
            query = rquery[at]
            both = jnp.concatenate(
                [jnp.where(first, query, 0.0), jnp.where(first, 0.0, query)], axis=1
            ).astype(jnp.bfloat16)
            scores = (
                lax.dot_general(
                    both, kv[p], (((1,), (1,)), ((), ())), preferred_element_type=jnp.float32
                )
                * inv_root
            )
            r = 2 * p
            limit = jnp.where(
                first_wide, 2 * lens[r // here, r % here],
                2 * lens[(r + 1) // here, (r + 1) % here],
            )
            scores = jnp.where(key_column < limit, scores, -1e30)
            new_score = new_scores[at]
            top = jnp.maximum(jnp.max(scores, axis=1, keepdims=True), new_score)
            weights = jnp.exp(scores - top)
            new_weight = jnp.exp(new_score - top)
            total = jnp.sum(weights, axis=1, keepdims=True) + new_weight
            moved = pltpu.roll(weights, 1, 1).astype(jnp.bfloat16)
            mixed = jnp.dot(moved, kv[p], preferred_element_type=jnp.float32)
            mixed = jnp.where(first, mixed[:, :HEAD_SIZE], mixed[:, HEAD_SIZE:])
            done.append((mixed + new_weight * value_new[at]) / total)
        attended = jnp.concatenate(done, axis=0).astype(jnp.bfloat16)
        att_send[c] = attended
        att_recv[c, me] = attended
        each(lambda d: spread(c, d, me).start())

    def fold(o):
        cols = pl.ds(o * o_chunk, o_chunk)
        return pltpu.make_async_remote_copy(
            src_ref=fold_s.at[:, cols], dst_ref=fold_r.at[:, cols],
            send_sem=fs_sem.at[o], recv_sem=fr_sem.at[o],
            device_id={"gy": across(0)}, device_id_type=MESH,
        )

    def cross(o, k):
        cols = pl.ds(o * o_chunk, o_chunk)
        return pltpu.make_async_remote_copy(
            src_ref=cross_s.at[k, :, cols], dst_ref=cross_r.at[k, :, cols],
            send_sem=cs_sem.at[k, o], recv_sem=cr_sem.at[k, o],
            device_id={"gy": across(k + 1)}, device_id_type=MESH,
        )

    def give(o):
        cols = pl.ds(o * o_chunk, o_chunk)
        return pltpu.make_async_remote_copy(
            src_ref=out.at[:, :, cols], dst_ref=out.at[:, :, cols],
            send_sem=os_sem.at[o], recv_sem=or_sem.at[o],
            device_id={"gy": across(0)}, device_id_type=MESH,
        )

    for c in range(nq):
        each(lambda d: spread(c, d, source(d)).wait_recv())
        x_f[...] = att_recv[c].astype(jnp.float32).reshape(n * group, HEAD_SIZE)
        for j in range(n):
            for b in range(batches):
                at = slice(b * rows + j * here, b * rows + (j + 1) * here)
                for h in range(hc):
                    x_s[at, h * HEAD_SIZE:(h + 1) * HEAD_SIZE] = x_f[
                        pl.ds(j * group + b * here * hc + h, here, stride=hc), :
                    ]
        xc = x_s[...].astype(jnp.bfloat16)
        wo_copy(c).wait()
        for o in range(no):
            cols = slice(o * o_chunk, (o + 1) * o_chunk)
            y = jnp.dot(
                xc, wo[c * q_chunk:(c + 1) * q_chunk, cols], preferred_element_type=jnp.float32
            )
            if c > 0:
                y = y + ybuf[:, cols]
            ybuf[:, cols] = y
            if c == nq - 1:
                @pl.when(follower)
                def _(o=o, cols=cols, y=y):
                    fold_s[:, cols] = y.astype(jnp.bfloat16)
                    fold(o).start()

    @pl.when(leader)
    def _():
        for o in range(no):
            cols = slice(o * o_chunk, (o + 1) * o_chunk)
            fold(o).wait_recv()
            y = ybuf[:, cols] + fold_r[:, cols].astype(jnp.float32)
            if bits > 1:
                cross_s[0, :, cols] = y.astype(jnp.bfloat16)
                cross(o, 0).start()
            else:
                ybuf[:, cols] = y
        for k in range(bits - 1):
            for o in range(no):
                cols = slice(o * o_chunk, (o + 1) * o_chunk)
                cross(o, k).wait_recv()
                y = cross_s[k, :, cols].astype(jnp.float32) + cross_r[k, :, cols].astype(jnp.float32)
                if k < bits - 2:
                    cross_s[k + 1, :, cols] = y.astype(jnp.bfloat16)
                    cross(o, k + 1).start()
                else:
                    y = y.reshape(batches, rows, o_chunk)
                    out[:, :, cols] = (tok[:, :, cols].astype(jnp.float32) + y).astype(jnp.bfloat16)
                    give(o).start()
        for o in range(no):
            for k in range(bits - 1):
                cross(o, k).wait_send()
            give(o).wait_send()

    @pl.when(follower)
    def _():
        for o in range(no):
            fold(o).wait_send()
        for o in range(no):
            give(o).wait_recv()

    for c in range(nq + 1):
        each(lambda d: shift(c, d, me).wait_send())
    for c in range(nq):
        each(lambda d: spread(c, d, me).wait_send())


def local(n, ny, tokens, lengths, norm_gain, w_query, key_value_weight, w_out, cache):
    batches, rows, depth = tokens.shape
    here = rows // n
    local_rows = batches * here
    q_width = w_query.shape[1]
    kv_heads = key_value_weight.shape[1]
    kv_width = kv_heads * key_value_weight.shape[2]
    assert kv_heads == 1 and ny >= 4 and ny & (ny - 1) == 0 and local_rows % 2 == 0
    heads = q_width // HEAD_SIZE
    out_width = w_out.shape[1]
    hc = 4
    splits = 2 if depth % 4096 == 0 else 1
    o_chunk = min(1024, out_width)
    nq, no = heads // hc, out_width // o_chunk
    assert nq * hc == heads
    bits = ny.bit_length() - 1
    freq = np.float32(ROPE_BASE) ** (
        -2.0 * np.arange(HEAD_SIZE // 2, dtype=np.float32) / HEAD_SIZE
    )
    freq = np.concatenate([freq, freq]).astype(np.float32)[None, :]
    positions = cache.shape[2] * 2
    interleaved = cache.reshape(local_rows * positions, HEAD_SIZE)
    hbm = pl.BlockSpec(memory_space=pltpu.HBM)
    f32, bf16 = jnp.float32, jnp.bfloat16
    dma = pltpu.SemaphoreType.DMA
    total_rows = batches * rows
    group = local_rows * hc
    return pl.pallas_call(
        functools.partial(kernel, n, ny, hc, splits, o_chunk),
        out_shape=pltpu.VMEM(tokens.shape, bf16),
        in_specs=[hbm] * 8,
        out_specs=pl.BlockSpec(memory_space=pltpu.VMEM),
        scratch_shapes=[
            pltpu.SMEM(lengths.shape, jnp.int32),
            pltpu.VMEM(tokens.shape, bf16),
            pltpu.VMEM((depth // HEAD_SIZE, HEAD_SIZE), bf16),
            pltpu.VMEM((1, HEAD_SIZE), f32),
            pltpu.VMEM(w_query.shape, bf16),
            pltpu.VMEM((depth, kv_width), bf16),
            pltpu.VMEM(w_out.shape, bf16),
            pltpu.VMEM((local_rows // 2, positions, 2 * HEAD_SIZE), bf16),
            pltpu.VMEM((total_rows, depth), bf16),
            pltpu.VMEM((nq, n, group, HEAD_SIZE), f32),
            pltpu.VMEM((nq, n, group, HEAD_SIZE), f32),
            pltpu.VMEM((n, local_rows, kv_width + HEAD_SIZE), f32),
            pltpu.VMEM((n, local_rows, kv_width + HEAD_SIZE), f32),
            pltpu.VMEM((nq, group, HEAD_SIZE), bf16),
            pltpu.VMEM((nq, n, group, HEAD_SIZE), bf16),
            pltpu.VMEM((n * group, HEAD_SIZE), f32),
            pltpu.VMEM((total_rows, hc * HEAD_SIZE), f32),
            pltpu.VMEM((total_rows, out_width), f32),
            pltpu.VMEM((total_rows, out_width), bf16),
            pltpu.VMEM((total_rows, out_width), bf16),
            pltpu.VMEM((bits - 1, total_rows, out_width), bf16),
            pltpu.VMEM((bits - 1, total_rows, out_width), bf16),
            dma((4,)), dma((nq, splits)), dma, dma((nq,)), dma((local_rows,)),
            dma((nq + 1, n)), dma((nq + 1, n)), dma((nq, n)), dma((nq, n)),
            dma((no,)), dma((no,)), dma((bits - 1, no)), dma((bits - 1, no)),
            dma((no,)), dma((no,)),
        ],
        compiler_params=pltpu.CompilerParams(
            collective_id=0, has_side_effects=True, vmem_limit_bytes=67043328 - 2 * tokens.size
        ),
    )(
        lengths, tokens, norm_gain.reshape(depth // HEAD_SIZE, HEAD_SIZE), jnp.asarray(freq),
        w_query, key_value_weight.reshape(depth, kv_width), w_out, interleaved,
    )


def solution(mesh):
    placed = (
        P(None, "groups", "gx"),
        P(None, ("groups", "gx")),
        P("gx"),
        P("gx", "gy"),
        P("gx", "gy", None),
        P("gy", "gx"),
        P(None, ("groups", "gx"), None, "gy", None, None),
    )
    return jax.shard_map(
        functools.partial(local, mesh.shape["gx"], mesh.shape["gy"]),
        mesh=mesh, in_specs=placed, out_specs=P(None, "groups", "gx"), check_vma=False,
    )
```

time: 28.5 us -> 38.3 us (1.34)
  Pallas kernels: 27.7 us -> 37.5 us
    pallas_call x1, Pallas kernels: 27.7 us -> 37.5 us  [local(): pl.pallas_call(functools.partial(kernel, n, ny, hc, splits, o_chunk), out...]
where the time goes in v1:
time: 38.3 us; the launch traced here: 38.2 us
  Pallas kernels  37.5 us (98%)
  local copies, waits for them, and re-layouts  0.66 us (2%)
    pallas_call x1, Pallas kernels, local(): pl.pallas_call(functools.partial(kernel, n, ny, hc, splits, o_chunk), out...  37.5 us

profile of v1, /device:TPU:0, one launch (start us, length us, event | category | flops | bytes accessed | tf_op | source)
XLA Modules:
  0.0 38.2 jit_solution(17206577552184833906)
XLA Ops:
  0.0 37.5 %shard_map.82 = bf16[2,8,4096]{2,1,0:T(8,128)(2,1)S(1)} custom-call(s32[2,2]{1,0:T(2,128)} %lens_hbm.1, bf16[2,8,4096]{2,1,0:T(8,128)(2,1)} %tok_hbm.1, bf16[32,128]{1,0:T(8,128)(2,1)} %bitcast.5, f32[1,128]{1,0:T(1,128)} %constant.2.clone.freq_hbm, bf16[4096,2048]{1,0:T(8,128)(2,1)} %wq_hbm.1, bf16[4096,256]{1,0:T(8,128)(2,1)} %bitcast.3, ...), custom_call_target="tpu_custom_call" | custom-call | tf_op jit(solution)/shard_map/pallas_call | solution.py:368
  37.5 0.7 %copy.10 = bf16[2,8,4096]{2,1,0:T(8,128)(2,1)} copy(bf16[2,8,4096]{2,1,0:T(8,128)(2,1)S(1)} %shard_map.82) | data formatting | bytes 262144

commit v2 on v1

v2 whole, which is shorter than its diff:
```python
import functools

import jax
import jax.numpy as jnp
import numpy as np
from jax import lax
from jax.experimental import pallas as pl
from jax.experimental.pallas import tpu as pltpu
from jax.sharding import PartitionSpec as P

MODEL_WIDTH = 16384
HEAD_SIZE = 128
ROPE_BASE = 500000.0
MESH = pl.DeviceIdType.MESH


def kernel(
    n, ny, chunks, splits, phases, ahead, outs,
    lens_hbm, tok_hbm, gain_hbm, freq_hbm, wq_hbm, wk_hbm, wo_hbm, kv_hbm,
    out,
    lens, tok, gain, freq, wq, wk, wo, kv, normed,
    acc, wide_s, keys, values, send, recv, q_s, o_s, att_send, att_recv, x_s,
    ybuf, y_send, y_recv,
    small_sem, stream_sem, wo_sem, kv_sem,
    qs_sem, qr_sem, as_sem, ar_sem, ys_sem, yr_sem, os_sem, or_sem,
):
    batches, rows, depth = tok.shape
    here = rows // n
    total_rows = batches * rows
    q_width = wq.shape[1]
    kv_width = wk.shape[1]
    out_width = wo.shape[1]
    local_rows = batches * here
    pairs = local_rows // 2
    positions = keys.shape[1]
    last = len(phases) - 1
    starts = [sum(phases[:i]) * HEAD_SIZE for i in range(len(phases))]
    widths = [heads * HEAD_SIZE for heads in phases]
    nc = len(chunks)
    q_starts = [sum(chunks[:i]) * HEAD_SIZE for i in range(nc)]
    q_widths = [heads * HEAD_SIZE for heads in chunks]
    me = lax.axis_index("gx")
    my = lax.axis_index("gy")
    leader = lax.rem(my, 2) == 1
    follower = lax.rem(my, 2) == 0

    small = [
        pltpu.make_async_copy(tok_hbm, tok, small_sem.at[0]),
        pltpu.make_async_copy(gain_hbm, gain, small_sem.at[1]),
        pltpu.make_async_copy(freq_hbm, freq, small_sem.at[2]),
        pltpu.make_async_copy(lens_hbm, lens, small_sem.at[3]),
    ]

    pieces = [(wk_hbm, wk)]
    for c in range(nc):
        part = depth // splits[c]
        for k in range(splits[c]):
            at = (pl.ds(k * part, part), pl.ds(q_starts[c], q_widths[c]))
            pieces.append((wq_hbm.at[at], wq.at[at]))

    def stream(i):
        return pltpu.make_async_copy(*pieces[i], stream_sem.at[i % ahead])

    kv_copy = pltpu.make_async_copy(kv_hbm, kv, kv_sem)

    def take(i):
        stream(i).wait()
        if i + ahead < len(pieces):
            stream(i + ahead).start()
        elif i + ahead == len(pieces):
            kv_copy.start()

    def wo_copy(c):
        at = pl.ds(starts[c], widths[c])
        return pltpu.make_async_copy(wo_hbm.at[at], wo.at[at], wo_sem.at[c])

    for copy in small:
        copy.start()
    for i in range(ahead):
        stream(i).start()

    barrier = pltpu.get_barrier_semaphore()

    def each(fn):
        if n <= 8:
            for d in range(1, n):
                fn(d)
        else:
            def body(d, carry):
                fn(d)
                return carry
            lax.fori_loop(1, n, body, 0)

    def greet(d):
        pl.semaphore_signal(
            barrier, inc=1, device_id={"gx": lax.rem(me + d, n)}, device_id_type=MESH
        )

    each(greet)

    for d in range(1, ny):
        pl.semaphore_signal(
            barrier, inc=1, device_id={"gy": lax.rem(my + d, ny)}, device_id_type=MESH
        )

    def to(d):
        return lax.rem(me + d, n)

    def drain(ref, sem):
        pltpu.make_async_copy(ref, ref, sem).wait()

    small[0].wait()
    small[1].wait()
    x = tok[...].astype(jnp.float32).reshape(total_rows, depth)
    for k in range(depth // HEAD_SIZE):
        cols = slice(k * HEAD_SIZE, (k + 1) * HEAD_SIZE)
        normed[:, cols] = (x[:, cols] * gain[k:k + 1, :].astype(jnp.float32)).astype(jnp.bfloat16)
    squares = jnp.broadcast_to(jnp.sum(x * x, axis=1, keepdims=True), (total_rows, HEAD_SIZE))

    def put(part, start):
        width = part.shape[1]
        for j in range(n):
            for b in range(batches):
                send[j, b * here:(b + 1) * here, start:start + width] = part[
                    b * rows + j * here:b * rows + (j + 1) * here, :
                ]

    def shift(c, start, width):
        cols = pl.ds(start, width)
        def one(d):
            pltpu.make_async_remote_copy(
                src_ref=send.at[to(d), :, cols], dst_ref=recv.at[me, :, cols],
                send_sem=qs_sem, recv_sem=qr_sem.at[c],
                device_id={"gx": to(d)}, device_id_type=MESH,
            ).start()
        each(one)

    def arrived(c, start, width):
        drain(recv.at[pl.ds(0, n - 1), :, pl.ds(start, width)], qr_sem.at[c])

    def summed(start, width):
        cols = pl.ds(start, width)
        def add(d, acc):
            return acc + recv[to(d), :, cols]
        return lax.fori_loop(1, n, add, send[me, :, cols], unroll=n <= 8)

    side = kv_width + HEAD_SIZE
    take(0)
    middle = depth // 2
    for k in range(2):
        ks = slice(k * middle, (k + 1) * middle)
        acc[:, k * kv_width:(k + 1) * kv_width] = jnp.dot(
            normed[:, ks], wk[ks], preferred_element_type=jnp.float32
        )
    for j in range(n):
        for b in range(batches):
            at = slice(b * rows + j * here, b * rows + (j + 1) * here)
            send[j, b * here:(b + 1) * here, q_width:q_width + kv_width] = (
                acc[at, :kv_width] + acc[at, kv_width:2 * kv_width]
            )
    put(squares, q_width + kv_width)
    i = 1
    for c in range(nc):
        size = depth // splits[c]
        for k in range(splits[c]):
            take(i)
            i += 1
            ks = slice(k * size, (k + 1) * size)
            half = q_widths[c] // 2
            for at in (0, half):
                piece = jnp.dot(
                    normed[:, ks], wq[ks, q_starts[c] + at:q_starts[c] + at + half],
                    preferred_element_type=jnp.float32,
                )
                if k > 0:
                    piece = piece + acc[:, at:at + half]
                if k < splits[c] - 1:
                    acc[:, at:at + half] = piece
                else:
                    put(piece, q_starts[c] + at)
        if c == 0:
            pl.semaphore_wait(barrier, n - 1 + ny - 1)
            shift(nc, q_width, side)
        shift(c, q_starts[c], q_widths[c])

    small[2].wait()
    small[3].wait()
    lane = lax.broadcasted_iota(jnp.int32, (local_rows, HEAD_SIZE), 1)
    row = lax.broadcasted_iota(jnp.int32, (local_rows, HEAD_SIZE), 0)
    place = jnp.zeros((local_rows, HEAD_SIZE), jnp.float32)
    for r in range(local_rows):
        place = jnp.where(row == r, lens[r // here, r % here].astype(jnp.float32), place)
    angle = place * freq[...]
    cosine = jnp.cos(angle)
    sine = jnp.sin(angle)
    sine = jnp.where(lane < HEAD_SIZE // 2, -sine, sine)

    def rotate(v):
        return v * cosine + pltpu.roll(v, HEAD_SIZE // 2, 1) * sine

    kv_copy.wait()
    for c in range(last + 1):
        wo_copy(c).start()
    block_rows = wide_s.shape[0]
    blocks = 2 * positions // block_rows

    def divide(t, carry):
        r = t // blocks
        wide_s[...] = kv[pl.ds(pl.multiple_of(t * block_rows, block_rows), block_rows), :].astype(
            jnp.float32
        )
        half = block_rows // 2
        at = pl.ds(pl.multiple_of(lax.rem(t, blocks) * half, half), half)
        lanes = pl.ds(pl.multiple_of(lax.rem(r, 2) * HEAD_SIZE, HEAD_SIZE), HEAD_SIZE)
        keys[r // 2, at, lanes] = wide_s[pl.ds(0, half, stride=2), :].astype(jnp.bfloat16)
        values[r // 2, at, lanes] = wide_s[pl.ds(1, half, stride=2), :].astype(jnp.bfloat16)
        return carry

    lax.fori_loop(0, local_rows * blocks, divide, 0)

    arrived(nc, q_width, side)
    tail = summed(q_width, side)
    scale = lax.rsqrt(tail[:, kv_width:] / MODEL_WIDTH + 1e-05)
    rkey = rotate(tail[:, :HEAD_SIZE] * scale)
    value_new = tail[:, HEAD_SIZE:2 * HEAD_SIZE] * scale
    inv_root = np.float32(1.0 / np.sqrt(np.float32(HEAD_SIZE)))

    def spread(c):
        cols = pl.ds(starts[c], widths[c])
        def one(d):
            pltpu.make_async_remote_copy(
                src_ref=att_send.at[:, cols], dst_ref=att_recv.at[me, :, cols],
                send_sem=as_sem, recv_sem=ar_sem.at[c],
                device_id={"gx": to(d)}, device_id_type=MESH,
            ).start()
        each(one)

    for c in range(last + 1):
        hc = phases[c]
        for i in range(nc):
            if starts[c] <= q_starts[i] < starts[c] + widths[c]:
                arrived(i, q_starts[i], q_widths[i])
        block = summed(starts[c], widths[c])
        for h in range(hc):
            q_s[pl.ds(h, local_rows, stride=hc), :] = rotate(
                block[:, h * HEAD_SIZE:(h + 1) * HEAD_SIZE] * scale
            )
        column = lax.broadcasted_iota(jnp.int32, (2 * hc, positions), 1)
        first = lax.broadcasted_iota(jnp.int32, (2 * hc, HEAD_SIZE), 0) < hc
        first_wide = lax.broadcasted_iota(jnp.int32, (2 * hc, positions), 0) < hc

        def pair_rows(v, p):
            shape = (2 * hc, v.shape[1])
            return jnp.where(
                first,
                jnp.broadcast_to(v[2 * p:2 * p + 1], shape),
                jnp.broadcast_to(v[2 * p + 1:2 * p + 2], shape),
            )

        weighed = []
        for p in range(pairs):
            query = q_s[p * 2 * hc:(p + 1) * 2 * hc, :].astype(jnp.bfloat16).astype(jnp.float32)
            both = jnp.concatenate(
                [jnp.where(first, query, 0.0), jnp.where(first, 0.0, query)], axis=1
            ).astype(jnp.bfloat16)
            scores = jnp.concatenate(
                [
                    lax.dot_general(
                        both, keys[p, at:at + positions // 2], (((1,), (1,)), ((), ())),
                        preferred_element_type=jnp.float32,
                    )
                    for at in (0, positions // 2)
                ],
                axis=1,
            ) * inv_root
            r = 2 * p
            limit = jnp.where(
                first_wide, lens[r // here, r % here], lens[(r + 1) // here, (r + 1) % here]
            )
            scores = jnp.where(column < limit, scores, -1e30)
            new_score = jnp.sum(query * pair_rows(rkey, p), axis=1, keepdims=True) * inv_root
            top = jnp.maximum(jnp.max(scores, axis=1, keepdims=True), new_score)
            weights = jnp.exp(scores - top)
            new_weight = jnp.exp(new_score - top)
            total = jnp.sum(weights, axis=1, keepdims=True) + new_weight
            weighed.append((weights.astype(jnp.bfloat16), new_weight, total))
        for p in range(pairs):
            weights, new_weight, total = weighed[p]
            mixed = sum(
                jnp.dot(
                    weights[:, at:at + positions // 2], values[p, at:at + positions // 2],
                    preferred_element_type=jnp.float32,
                )
                for at in (0, positions // 2)
            )
            mixed = jnp.where(first, mixed[:, :HEAD_SIZE], mixed[:, HEAD_SIZE:])
            o_s[p * 2 * hc:(p + 1) * 2 * hc, :] = (
                mixed + new_weight * pair_rows(value_new, p)
            ) / total
        for h in range(hc):
            cols = slice(starts[c] + h * HEAD_SIZE, starts[c] + (h + 1) * HEAD_SIZE)
            att_send[:, cols] = o_s[pl.ds(h, local_rows, stride=hc), :].astype(jnp.bfloat16)
        spread(c)

    partner = my + 1 - 2 * lax.rem(my, 2)
    far = lax.rem(my + 2, 4)
    far_leader = far + 1 - lax.rem(far, 2)

    leading = lax.rem(my, 2)

    def hand(o, slot, target):
        cols = pl.ds(*outs[o])
        return pltpu.make_async_remote_copy(
            src_ref=y_send.at[:, cols], dst_ref=y_recv.at[slot, :, cols],
            send_sem=ys_sem.at[lax.rem(slot, 2)], recv_sem=yr_sem.at[slot, o],
            device_id={"gy": target}, device_id_type=MESH,
        )

    def give(o):
        cols = pl.ds(*outs[o])
        return pltpu.make_async_remote_copy(
            src_ref=out.at[:, :, cols], dst_ref=out.at[:, :, cols],
            send_sem=os_sem, recv_sem=or_sem,
            device_id={"gy": partner}, device_id_type=MESH,
        )

    for c in range(last + 1):
        fs = slice(starts[c], starts[c] + widths[c])
        drain(att_recv.at[pl.ds(0, n - 1), :, pl.ds(starts[c], widths[c])], ar_sem.at[c])
        att_recv[me, :, fs] = att_send[:, fs]
        for j in range(n):
            block = att_recv[j, :, fs].astype(jnp.float32)
            for b in range(batches):
                x_s[b * rows + j * here:b * rows + (j + 1) * here, :widths[c]] = block[
                    b * here:(b + 1) * here, :
                ]
        xc = x_s[:, :widths[c]].astype(jnp.bfloat16)
        wo_copy(c).wait()
        for o in range(len(outs)):
            cols = slice(outs[o][0], outs[o][0] + outs[o][1])
            half = outs[o][1] // 2
            for at in (cols.start, cols.start + half):
                part = slice(at, at + half)
                y = jnp.dot(xc, wo[fs, part], preferred_element_type=jnp.float32)
                if c > 0:
                    y = y + ybuf[:, part]
                if c < last:
                    ybuf[:, part] = y
                else:
                    y_send[:, part] = y.astype(jnp.bfloat16)
            if c == last:
                hand(o, 1 - leading, far_leader).start()

    @pl.when(leader)
    def _():
        for o in range(len(outs)):
            cols = slice(outs[o][0], outs[o][0] + outs[o][1])
            for slot in (0, 2, 1):
                hand(o, slot, far).wait_recv()
            parts = [y_recv[slot, :, cols].astype(jnp.float32) for slot in range(3)]
            y = (y_send[:, cols].astype(jnp.float32) + parts[0]) + (parts[1] + parts[2])
            y = y.reshape(batches, rows, outs[o][1])
            out[:, :, cols] = (tok[:, :, cols].astype(jnp.float32) + y).astype(jnp.bfloat16)
            give(o).start()
        drain(out, os_sem)

    @pl.when(follower)
    def _():
        for o in range(len(outs)):
            hand(o, 2, partner).start()
        drain(y_send, ys_sem.at[0])
        drain(out, or_sem)

    drain(y_send, ys_sem.at[1 - leading])
    drain(send.at[pl.ds(0, n - 1)], qs_sem)
    drain(att_recv.at[pl.ds(0, n - 1)], as_sem)


def local(n, ny, tokens, lengths, norm_gain, w_query, key_value_weight, w_out, cache):
    batches, rows, depth = tokens.shape
    here = rows // n
    local_rows = batches * here
    q_width = w_query.shape[1]
    kv_heads = key_value_weight.shape[1]
    kv_width = kv_heads * key_value_weight.shape[2]
    assert kv_heads == 1 and ny == 4 and local_rows % 2 == 0
    heads = q_width // HEAD_SIZE
    out_width = w_out.shape[1]
    quarter = heads // 4
    chunks = (quarter,) * 4
    phases = (2 * quarter, quarter, quarter)
    splits = tuple(max(1, depth * p * HEAD_SIZE // (1 << 20)) for p in chunks)
    ahead = 4
    step = max(out_width // 8, 2 * HEAD_SIZE)
    outs = [(0, step)]
    while outs[-1][0] + outs[-1][1] < out_width:
        start = sum(outs[-1])
        outs.append((start, step if start < 2 * step else 2 * step))
    freq = np.float32(ROPE_BASE) ** (
        -2.0 * np.arange(HEAD_SIZE // 2, dtype=np.float32) / HEAD_SIZE
    )
    freq = np.concatenate([freq, freq]).astype(np.float32)[None, :]
    positions = cache.shape[2]
    interleaved = cache.reshape(local_rows * positions * 2, HEAD_SIZE)
    hbm = pl.BlockSpec(memory_space=pltpu.HBM)
    f32, bf16 = jnp.float32, jnp.bfloat16
    dma = pltpu.SemaphoreType.DMA
    total_rows = batches * rows
    wide = q_width + kv_width + HEAD_SIZE
    most = max(phases)
    return pl.pallas_call(
        functools.partial(kernel, n, ny, chunks, splits, phases, ahead, outs),
        out_shape=pltpu.VMEM(tokens.shape, bf16),
        in_specs=[hbm] * 8,
        out_specs=pl.BlockSpec(memory_space=pltpu.VMEM),
        scratch_shapes=[
            pltpu.SMEM(lengths.shape, jnp.int32),
            pltpu.VMEM(tokens.shape, bf16),
            pltpu.VMEM((depth // HEAD_SIZE, HEAD_SIZE), bf16),
            pltpu.VMEM((1, HEAD_SIZE), f32),
            pltpu.VMEM(w_query.shape, bf16),
            pltpu.VMEM((depth, kv_width), bf16),
            pltpu.VMEM(w_out.shape, bf16),
            pltpu.VMEM(interleaved.shape, bf16),
            pltpu.VMEM((total_rows, depth), bf16),
            pltpu.VMEM((total_rows, most * HEAD_SIZE), f32),
            pltpu.VMEM((positions, HEAD_SIZE), f32),
            pltpu.VMEM((local_rows // 2, positions, 2 * HEAD_SIZE), bf16),
            pltpu.VMEM((local_rows // 2, positions, 2 * HEAD_SIZE), bf16),
            pltpu.VMEM((n, local_rows, wide), f32),
            pltpu.VMEM((n, local_rows, wide), f32),
            pltpu.VMEM((local_rows * most, HEAD_SIZE), f32),
            pltpu.VMEM((local_rows * most, HEAD_SIZE), f32),
            pltpu.VMEM((local_rows, q_width), bf16),
            pltpu.VMEM((n, local_rows, q_width), bf16),
            pltpu.VMEM((total_rows, most * HEAD_SIZE), f32),
            pltpu.VMEM((total_rows, out_width), f32),
            pltpu.VMEM((total_rows, out_width), bf16),
            pltpu.VMEM((3, total_rows, out_width), bf16),
            dma((4,)), dma((ahead,)), dma((len(phases),)), dma,
            dma, dma((len(chunks) + 1,)), dma, dma((len(phases),)),
            dma((2,)), dma((3, len(outs))), dma, dma,
        ],
        compiler_params=pltpu.CompilerParams(
            collective_id=0, has_side_effects=True, vmem_limit_bytes=67043328 - 2 * tokens.size
        ),
    )(
        lengths, tokens, norm_gain.reshape(depth // HEAD_SIZE, HEAD_SIZE), jnp.asarray(freq),
        w_query, key_value_weight.reshape(depth, kv_width), w_out, interleaved,
    )


def solution(mesh):
    placed = (
        P(None, "groups", "gx"),
        P(None, ("groups", "gx")),
        P("gx"),
        P("gx", "gy"),
        P("gx", "gy", None),
        P("gy", "gx"),
        P(None, ("groups", "gx"), None, "gy", None, None),
    )
    return jax.shard_map(
        functools.partial(local, mesh.shape["gx"], mesh.shape["gy"]),
        mesh=mesh, in_specs=placed, out_specs=P(None, "groups", "gx"), check_vma=False,
    )
```

time: 38.3 us -> 23.7 us (0.62)
  Pallas kernels: 37.5 us -> 22.9 us
    pallas_call x1, Pallas kernels: 37.5 us -> 22.9 us  [local(): pl.pallas_call(functools.partial(kernel, n, ny, chunks, splits, phases, a...]
where the time goes in v2:
time: 23.7 us; the launch traced here: 23.6 us
  Pallas kernels  22.9 us (97%)
  local copies, waits for them, and re-layouts  0.66 us (3%)
    pallas_call x1, Pallas kernels, local(): pl.pallas_call(functools.partial(kernel, n, ny, chunks, splits, phases, a...  22.9 us
    unnamed x1, local copies, waits for them, and re-layouts  0.66 us

profile of v2, /device:TPU:0, one launch (start us, length us, event | category | flops | bytes accessed | tf_op | source)
XLA Modules:
  0.0 23.6 jit_solution(10456238159531902728)
XLA Ops:
  0.0 22.9 %shard_map.82 = bf16[2,8,4096]{2,1,0:T(8,128)(2,1)S(1)} custom-call(s32[2,2]{1,0:T(2,128)} %lens_hbm.1, bf16[2,8,4096]{2,1,0:T(8,128)(2,1)} %tok_hbm.1, bf16[32,128]{1,0:T(8,128)(2,1)} %bitcast.5, f32[1,128]{1,0:T(1,128)} %constant.2.clone.freq_hbm, bf16[4096,2048]{1,0:T(8,128)(2,1)} %wq_hbm.1, bf16[4096,256]{1,0:T(8,128)(2,1)} %bitcast.3, ...), custom_call_target="tpu_custom_call" | custom-call | tf_op jit(solution)/shard_map/pallas_call | solution.py:411
  22.9 0.7 %copy.10 = bf16[2,8,4096]{2,1,0:T(8,128)(2,1)} copy(bf16[2,8,4096]{2,1,0:T(8,128)(2,1)S(1)} %shard_map.82) | data formatting | bytes 262144

commit v3 on v2

--- a/solution.py
+++ b/solution.py
@@ -21,8 +21,7 @@
     lens, tok, gain, freq, wq, wk, wo, kv, normed,
     acc, wide_s, keys, values, send, recv, q_s, o_s, att_send, att_recv, x_s,
     ybuf, y_send, y_recv,
-    small_sem, stream_sem, wo_sem, kv_sem,
-    qs_sem, qr_sem, as_sem, ar_sem, ys_sem, yr_sem, os_sem, or_sem,
+    small_sem, stream_sem, qs_sem, qr_sem, as_sem, ar_sem, ys_sem, yr_sem, out_sem,
 ):
     batches, rows, depth = tok.shape
     here = rows // n
@@ -53,26 +52,25 @@
 
     pieces = [(wk_hbm, wk)]
     for c in range(nc):
-        part = depth // splits[c]
-        for k in range(splits[c]):
-            at = (pl.ds(k * part, part), pl.ds(q_starts[c], q_widths[c]))
+        for begin, end in splits[c]:
+            at = (pl.ds(begin, end - begin), pl.ds(q_starts[c], q_widths[c]))
             pieces.append((wq_hbm.at[at], wq.at[at]))
+
+    for r in range(local_rows):
+        at = pl.ds(r * 2 * positions, 2 * positions)
+        pieces.append((kv_hbm.at[at], kv.at[at]))
 
     def stream(i):
         return pltpu.make_async_copy(*pieces[i], stream_sem.at[i % ahead])
-
-    kv_copy = pltpu.make_async_copy(kv_hbm, kv, kv_sem)
 
     def take(i):
         stream(i).wait()
         if i + ahead < len(pieces):
             stream(i + ahead).start()
-        elif i + ahead == len(pieces):
-            kv_copy.start()
 
     def wo_copy(c):
         at = pl.ds(starts[c], widths[c])
-        return pltpu.make_async_copy(wo_hbm.at[at], wo.at[at], wo_sem.at[c])
+        return pltpu.make_async_copy(wo_hbm.at[at], wo.at[at], stream_sem.at[c])
 
     for copy in small:
         copy.start()
@@ -125,6 +123,14 @@
                     b * rows + j * here:b * rows + (j + 1) * here, :
                 ]
 
+    def put_halves(start, width):
+        for j in range(n):
+            for b in range(batches):
+                at = slice(b * rows + j * here, b * rows + (j + 1) * here)
+                send[j, b * here:(b + 1) * here, start:start + width] = (
+                    acc[at, :width] + acc[at, width:2 * width]
+                )
+
     def shift(c, start, width):
         cols = pl.ds(start, width)
         def one(d):
@@ -152,32 +158,32 @@
         acc[:, k * kv_width:(k + 1) * kv_width] = jnp.dot(
             normed[:, ks], wk[ks], preferred_element_type=jnp.float32
         )
-    for j in range(n):
-        for b in range(batches):
-            at = slice(b * rows + j * here, b * rows + (j + 1) * here)
-            send[j, b * here:(b + 1) * here, q_width:q_width + kv_width] = (
-                acc[at, :kv_width] + acc[at, kv_width:2 * kv_width]
-            )
+    put_halves(q_width, kv_width)
     put(squares, q_width + kv_width)
     i = 1
     for c in range(nc):
-        size = depth // splits[c]
-        for k in range(splits[c]):
+        for k, (begin, end) in enumerate(splits[c]):
             take(i)
             i += 1
-            ks = slice(k * size, (k + 1) * size)
-            half = q_widths[c] // 2
-            for at in (0, half):
+            narrow = q_widths[c] == 2 * HEAD_SIZE
+            half = q_widths[c] if narrow else q_widths[c] // 2
+            size = (end - begin) // 2 if narrow else end - begin
+            for m in range(2):
+                at = 0 if narrow else m * half
+                ks = slice(begin + m * size, begin + (m + 1) * size) if narrow else slice(begin, end)
                 piece = jnp.dot(
                     normed[:, ks], wq[ks, q_starts[c] + at:q_starts[c] + at + half],
                     preferred_element_type=jnp.float32,
                 )
+                into = slice(m * half, (m + 1) * half)
                 if k > 0:
-                    piece = piece + acc[:, at:at + half]
-                if k < splits[c] - 1:
-                    acc[:, at:at + half] = piece
+                    piece = piece + acc[:, into]
+                if narrow or k < len(splits[c]) - 1:
+                    acc[:, into] = piece
                 else:
                     put(piece, q_starts[c] + at)
+        if narrow:
+            put_halves(q_starts[c], half)
         if c == 0:
             pl.semaphore_wait(barrier, n - 1 + ny - 1)
             shift(nc, q_width, side)
@@ -198,9 +204,6 @@
     def rotate(v):
         return v * cosine + pltpu.roll(v, HEAD_SIZE // 2, 1) * sine
 
-    kv_copy.wait()
-    for c in range(last + 1):
-        wo_copy(c).start()
     block_rows = wide_s.shape[0]
     blocks = 2 * positions // block_rows
 
@@ -216,7 +219,12 @@
         values[r // 2, at, lanes] = wide_s[pl.ds(1, half, stride=2), :].astype(jnp.bfloat16)
         return carry
 
-    lax.fori_loop(0, local_rows * blocks, divide, 0)
+    for r in range(local_rows):
+        take(i)
+        i += 1
+        lax.fori_loop(r * blocks, (r + 1) * blocks, divide, 0)
+    for c in range(last + 1):
+        wo_copy(c).start()
 
     arrived(nc, q_width, side)
     tail = summed(q_width, side)
@@ -237,9 +245,9 @@
 
     for c in range(last + 1):
         hc = phases[c]
-        for i in range(nc):
-            if starts[c] <= q_starts[i] < starts[c] + widths[c]:
-                arrived(i, q_starts[i], q_widths[i])
+        for k in range(nc):
+            if starts[c] <= q_starts[k] < starts[c] + widths[c]:
+                arrived(k, q_starts[k], q_widths[k])
         block = summed(starts[c], widths[c])
         for h in range(hc):
             q_s[pl.ds(h, local_rows, stride=hc), :] = rotate(
@@ -306,13 +314,11 @@
     far = lax.rem(my + 2, 4)
     far_leader = far + 1 - lax.rem(far, 2)
 
-    leading = lax.rem(my, 2)
-
     def hand(o, slot, target):
         cols = pl.ds(*outs[o])
         return pltpu.make_async_remote_copy(
             src_ref=y_send.at[:, cols], dst_ref=y_recv.at[slot, :, cols],
-            send_sem=ys_sem.at[lax.rem(slot, 2)], recv_sem=yr_sem.at[slot, o],
+            send_sem=ys_sem, recv_sem=yr_sem.at[o],
             device_id={"gy": target}, device_id_type=MESH,
         )
 
@@ -320,9 +326,15 @@
         cols = pl.ds(*outs[o])
         return pltpu.make_async_remote_copy(
             src_ref=out.at[:, :, cols], dst_ref=out.at[:, :, cols],
-            send_sem=os_sem, recv_sem=or_sem,
+            send_sem=out_sem, recv_sem=out_sem,
             device_id={"gy": partner}, device_id_type=MESH,
         )
+
+    def product(o, fs, xc):
+        start, width = outs[o]
+        for at in (start, start + width // 2):
+            part = slice(at, at + width // 2)
+            yield part, jnp.dot(xc, wo[fs, part], preferred_element_type=jnp.float32)
 
     for c in range(last + 1):
         fs = slice(starts[c], starts[c] + widths[c])
@@ -336,42 +348,35 @@
                 ]
         xc = x_s[:, :widths[c]].astype(jnp.bfloat16)
         wo_copy(c).wait()
-        for o in range(len(outs)):
-            cols = slice(outs[o][0], outs[o][0] + outs[o][1])
-            half = outs[o][1] // 2
-            for at in (cols.start, cols.start + half):
-                part = slice(at, at + half)
-                y = jnp.dot(xc, wo[fs, part], preferred_element_type=jnp.float32)
-                if c > 0:
-                    y = y + ybuf[:, part]
-                if c < last:
-                    ybuf[:, part] = y
-                else:
-                    y_send[:, part] = y.astype(jnp.bfloat16)
-            if c == last:
-                hand(o, 1 - leading, far_leader).start()
+        if c < last:
+            for o in range(len(outs)):
+                for part, y in product(o, fs, xc):
+                    ybuf[:, part] = y + ybuf[:, part] if c > 0 else y
+
+    for o in range(len(outs)):
+        for part, y in product(o, fs, xc):
+            y_send[:, part] = (y + ybuf[:, part]).astype(jnp.bfloat16)
+        hand(o, 1 - lax.rem(my, 2), far_leader).start()
 
     @pl.when(leader)
     def _():
         for o in range(len(outs)):
             cols = slice(outs[o][0], outs[o][0] + outs[o][1])
-            for slot in (0, 2, 1):
-                hand(o, slot, far).wait_recv()
+            drain(y_recv.at[:, :, cols], yr_sem.at[o])
             parts = [y_recv[slot, :, cols].astype(jnp.float32) for slot in range(3)]
             y = (y_send[:, cols].astype(jnp.float32) + parts[0]) + (parts[1] + parts[2])
             y = y.reshape(batches, rows, outs[o][1])
             out[:, :, cols] = (tok[:, :, cols].astype(jnp.float32) + y).astype(jnp.bfloat16)
             give(o).start()
-        drain(out, os_sem)
+        drain(y_send, ys_sem)
 
     @pl.when(follower)
     def _():
         for o in range(len(outs)):
             hand(o, 2, partner).start()
-        drain(y_send, ys_sem.at[0])
-        drain(out, or_sem)
-
-    drain(y_send, ys_sem.at[1 - leading])
+        drain(y_recv.at[0:2], ys_sem)
+
+    drain(out, out_sem)
     drain(send.at[pl.ds(0, n - 1)], qs_sem)
     drain(att_recv.at[pl.ds(0, n - 1)], as_sem)
 
@@ -387,15 +392,21 @@
     heads = q_width // HEAD_SIZE
     out_width = w_out.shape[1]
     quarter = heads // 4
-    chunks = (quarter,) * 4
-    phases = (2 * quarter, quarter, quarter)
-    splits = tuple(max(1, depth * p * HEAD_SIZE // (1 << 20)) for p in chunks)
+    chunks = (quarter,) * 3 + (quarter // 2,) * 2
+    phases = (2 * quarter, 2 * quarter)
+    cuts = []
+    for c, width in enumerate(chunks):
+        parts = max(1, depth * width * HEAD_SIZE >> 20)
+        size = depth // parts
+        cut = [(k * size, (k + 1) * size) for k in range(parts)]
+        if c == len(chunks) - 1 and size % 512 == 0:
+            begin, end = cut.pop()
+            middle = (begin + end) // 2
+            cut += [(begin, middle), (middle, end)]
+        cuts.append(cut)
     ahead = 4
-    step = max(out_width // 8, 2 * HEAD_SIZE)
-    outs = [(0, step)]
-    while outs[-1][0] + outs[-1][1] < out_width:
-        start = sum(outs[-1])
-        outs.append((start, step if start < 2 * step else 2 * step))
+    step = min(1024, out_width)
+    outs = [(start, step) for start in range(0, out_width, step)]
     freq = np.float32(ROPE_BASE) ** (
         -2.0 * np.arange(HEAD_SIZE // 2, dtype=np.float32) / HEAD_SIZE
     )
@@ -409,7 +420,7 @@
     wide = q_width + kv_width + HEAD_SIZE
     most = max(phases)
     return pl.pallas_call(
-        functools.partial(kernel, n, ny, chunks, splits, phases, ahead, outs),
+        functools.partial(kernel, n, ny, chunks, cuts, phases, ahead, outs),
         out_shape=pltpu.VMEM(tokens.shape, bf16),
         in_specs=[hbm] * 8,
         out_specs=pl.BlockSpec(memory_space=pltpu.VMEM),
@@ -437,9 +448,8 @@
             pltpu.VMEM((total_rows, out_width), f32),
             pltpu.VMEM((total_rows, out_width), bf16),
             pltpu.VMEM((3, total_rows, out_width), bf16),
-            dma((4,)), dma((ahead,)), dma((len(phases),)), dma,
-            dma, dma((len(chunks) + 1,)), dma, dma((len(phases),)),
-            dma((2,)), dma((3, len(outs))), dma, dma,
+            dma((4,)), dma((ahead,)), dma, dma((len(chunks) + 1,)),
+            dma, dma((len(phases),)), dma, dma((len(outs),)), dma,
         ],
         compiler_params=pltpu.CompilerParams(
             collective_id=0, has_side_effects=True, vmem_limit_bytes=67043328 - 2 * tokens.size

time: 23.7 us -> 23.3 us (0.983)
  Pallas kernels: 22.9 us -> 22.5 us
    pallas_call x1, Pallas kernels: 22.9 us -> 22.5 us  [local(): pl.pallas_call(functools.partial(kernel, n, ny, chunks, cuts, phases, ahe...]
where the time goes in v3:
time: 23.3 us; the launch traced here: 23.2 us
  Pallas kernels  22.5 us (97%)
  local copies, waits for them, and re-layouts  0.66 us (3%)
    pallas_call x1, Pallas kernels, local(): pl.pallas_call(functools.partial(kernel, n, ny, chunks, cuts, phases, ahe...  22.5 us
    unnamed x1, local copies, waits for them, and re-layouts  0.66 us

profile of v3, /device:TPU:0, one launch (start us, length us, event | category | flops | bytes accessed | tf_op | source)
XLA Modules:
  0.0 23.2 jit_solution(3793363396819114030)
XLA Ops:
  0.0 22.5 %shard_map.82 = bf16[2,8,4096]{2,1,0:T(8,128)(2,1)S(1)} custom-call(s32[2,2]{1,0:T(2,128)} %lens_hbm.1, bf16[2,8,4096]{2,1,0:T(8,128)(2,1)} %tok_hbm.1, bf16[32,128]{1,0:T(8,128)(2,1)} %bitcast.5, f32[1,128]{1,0:T(1,128)} %constant.2.clone.freq_hbm, bf16[4096,2048]{1,0:T(8,128)(2,1)} %wq_hbm.1, bf16[4096,256]{1,0:T(8,128)(2,1)} %bitcast.3, ...), custom_call_target="tpu_custom_call" | custom-call | tf_op jit(solution)/shard_map/pallas_call | solution.py:422
  22.5 0.7 %copy.10 = bf16[2,8,4096]{2,1,0:T(8,128)(2,1)} copy(bf16[2,8,4096]{2,1,0:T(8,128)(2,1)S(1)} %shard_map.82) | data formatting | bytes 262144

commit v4 on v3

--- a/solution.py
+++ b/solution.py
@@ -313,12 +313,16 @@
     partner = my + 1 - 2 * lax.rem(my, 2)
     far = lax.rem(my + 2, 4)
     far_leader = far + 1 - lax.rem(far, 2)
+    far_other = far + 1 - 2 * lax.rem(far, 2)
+    final = len(outs) - 1
+    final_cols = pl.ds(*outs[final])
+    early_cols = pl.ds(0, outs[final][0])
 
     def hand(o, slot, target):
         cols = pl.ds(*outs[o])
         return pltpu.make_async_remote_copy(
             src_ref=y_send.at[:, cols], dst_ref=y_recv.at[slot, :, cols],
-            send_sem=ys_sem, recv_sem=yr_sem.at[o],
+            send_sem=ys_sem.at[o // final if final else 1], recv_sem=yr_sem.at[o],
             device_id={"gy": target}, device_id_type=MESH,
         )
 
@@ -356,27 +360,45 @@
     for o in range(len(outs)):
         for part, y in product(o, fs, xc):
             y_send[:, part] = (y + ybuf[:, part]).astype(jnp.bfloat16)
-        hand(o, 1 - lax.rem(my, 2), far_leader).start()
-
-    @pl.when(leader)
-    def _():
-        for o in range(len(outs)):
-            cols = slice(outs[o][0], outs[o][0] + outs[o][1])
-            drain(y_recv.at[:, :, cols], yr_sem.at[o])
-            parts = [y_recv[slot, :, cols].astype(jnp.float32) for slot in range(3)]
-            y = (y_send[:, cols].astype(jnp.float32) + parts[0]) + (parts[1] + parts[2])
-            y = y.reshape(batches, rows, outs[o][1])
-            out[:, :, cols] = (tok[:, :, cols].astype(jnp.float32) + y).astype(jnp.bfloat16)
-            give(o).start()
-        drain(y_send, ys_sem)
-
-    @pl.when(follower)
-    def _():
-        for o in range(len(outs)):
+        if o < final:
+            hand(o, 1 - lax.rem(my, 2), far_leader).start()
+        else:
+            hand(o, 0, far).start()
+            hand(o, 1, far_other).start()
             hand(o, 2, partner).start()
-        drain(y_recv.at[0:2], ys_sem)
-
-    drain(out, out_sem)
+
+    def total(o):
+        cols = slice(outs[o][0], outs[o][0] + outs[o][1])
+        drain(y_recv.at[:, :, cols], yr_sem.at[o])
+        parts = [y_recv[slot, :, cols].astype(jnp.float32) for slot in range(3)]
+        y = (y_send[:, cols].astype(jnp.float32) + parts[0]) + (parts[1] + parts[2])
+        y = y.reshape(batches, rows, outs[o][1])
+        out[:, :, cols] = (tok[:, :, cols].astype(jnp.float32) + y).astype(jnp.bfloat16)
+
+    if final:
+        @pl.when(leader)
+        def _():
+            for o in range(final):
+                total(o)
+                give(o).start()
+
+        @pl.when(follower)
+        def _():
+            for o in range(final):
+                hand(o, 2, partner).start()
+
+    total(final)
+    if final:
+        @pl.when(leader)
+        def _():
+            drain(y_send.at[:, early_cols], ys_sem.at[0])
+
+        @pl.when(follower)
+        def _():
+            drain(y_recv.at[0:2, :, early_cols], ys_sem.at[0])
+
+        drain(out.at[:, :, early_cols], out_sem)
+    drain(y_recv.at[:, :, final_cols], ys_sem.at[1])
     drain(send.at[pl.ds(0, n - 1)], qs_sem)
     drain(att_recv.at[pl.ds(0, n - 1)], as_sem)
 
@@ -449,7 +471,7 @@
             pltpu.VMEM((total_rows, out_width), bf16),
             pltpu.VMEM((3, total_rows, out_width), bf16),
             dma((4,)), dma((ahead,)), dma, dma((len(chunks) + 1,)),
-            dma, dma((len(phases),)), dma, dma((len(outs),)), dma,
+            dma, dma((len(phases),)), dma((2,)), dma((len(outs),)), dma,
         ],
         compiler_params=pltpu.CompilerParams(
             collective_id=0, has_side_effects=True, vmem_limit_bytes=67043328 - 2 * tokens.size

time: 23.3 us -> 22.9 us (0.983)
  Pallas kernels: 22.5 us -> 22.1 us
    pallas_call x1, Pallas kernels: 22.5 us -> 22.1 us  [local(): pl.pallas_call(functools.partial(kernel, n, ny, chunks, cuts, phases, ahe...]
where the time goes in v4:
time: 22.9 us; the launch traced here: 22.8 us
  Pallas kernels  22.1 us (97%)
  local copies, waits for them, and re-layouts  0.66 us (3%)
    pallas_call x1, Pallas kernels, local(): pl.pallas_call(functools.partial(kernel, n, ny, chunks, cuts, phases, ahe...  22.1 us
    unnamed x1, local copies, waits for them, and re-layouts  0.66 us

profile of v4, /device:TPU:0, one launch (start us, length us, event | category | flops | bytes accessed | tf_op | source)
XLA Modules:
  0.0 22.8 jit_solution(9258413252667393936)
XLA Ops:
  0.0 22.1 %shard_map.82 = bf16[2,8,4096]{2,1,0:T(8,128)(2,1)S(1)} custom-call(s32[2,2]{1,0:T(2,128)} %lens_hbm.1, bf16[2,8,4096]{2,1,0:T(8,128)(2,1)} %tok_hbm.1, bf16[32,128]{1,0:T(8,128)(2,1)} %bitcast.5, f32[1,128]{1,0:T(1,128)} %constant.2.clone.freq_hbm, bf16[4096,2048]{1,0:T(8,128)(2,1)} %wq_hbm.1, bf16[4096,256]{1,0:T(8,128)(2,1)} %bitcast.3, ...), custom_call_target="tpu_custom_call" | custom-call | tf_op jit(solution)/shard_map/pallas_call | solution.py:444
  22.1 0.7 %copy.10 = bf16[2,8,4096]{2,1,0:T(8,128)(2,1)} copy(bf16[2,8,4096]{2,1,0:T(8,128)(2,1)S(1)} %shard_map.82) | data formatting | bytes 262144

commit v5 on v4

--- a/solution.py
+++ b/solution.py
@@ -70,7 +70,7 @@
 
     def wo_copy(c):
         at = pl.ds(starts[c], widths[c])
-        return pltpu.make_async_copy(wo_hbm.at[at], wo.at[at], stream_sem.at[c])
+        return pltpu.make_async_copy(wo_hbm.at[at], wo.at[at], small_sem.at[c])
 
     for copy in small:
         copy.start()
@@ -131,12 +131,15 @@
                     acc[at, :width] + acc[at, width:2 * width]
                 )
 
-    def shift(c, start, width):
+    def stage(start):
+        return sum(start >= begin for begin in starts[1:] + [q_width])
+
+    def shift(start, width):
         cols = pl.ds(start, width)
         def one(d):
             pltpu.make_async_remote_copy(
                 src_ref=send.at[to(d), :, cols], dst_ref=recv.at[me, :, cols],
-                send_sem=qs_sem, recv_sem=qr_sem.at[c],
+                send_sem=qs_sem, recv_sem=qr_sem.at[stage(start)],
                 device_id={"gx": to(d)}, device_id_type=MESH,
             ).start()
         each(one)
@@ -186,8 +189,8 @@
             put_halves(q_starts[c], half)
         if c == 0:
             pl.semaphore_wait(barrier, n - 1 + ny - 1)
-            shift(nc, q_width, side)
-        shift(c, q_starts[c], q_widths[c])
+            shift(q_width, side)
+        shift(q_starts[c], q_widths[c])
 
     small[2].wait()
     small[3].wait()
@@ -204,33 +207,47 @@
     def rotate(v):
         return v * cosine + pltpu.roll(v, HEAD_SIZE // 2, 1) * sine
 
-    block_rows = wide_s.shape[0]
+    block_rows = wide_s.shape[1]
     blocks = 2 * positions // block_rows
-
-    def divide(t, carry):
-        r = t // blocks
-        wide_s[...] = kv[pl.ds(pl.multiple_of(t * block_rows, block_rows), block_rows), :].astype(
-            jnp.float32
-        )
-        half = block_rows // 2
-        at = pl.ds(pl.multiple_of(lax.rem(t, blocks) * half, half), half)
-        lanes = pl.ds(pl.multiple_of(lax.rem(r, 2) * HEAD_SIZE, HEAD_SIZE), HEAD_SIZE)
-        keys[r // 2, at, lanes] = wide_s[pl.ds(0, half, stride=2), :].astype(jnp.bfloat16)
-        values[r // 2, at, lanes] = wide_s[pl.ds(1, half, stride=2), :].astype(jnp.bfloat16)
-        return carry
-
-    for r in range(local_rows):
+    half_rows = block_rows // 2
+
+    def divide(r):
+        lanes = slice((r % 2) * HEAD_SIZE, (r % 2 + 1) * HEAD_SIZE)
+        for t in range(blocks):
+            start = (r * blocks + t) * block_rows
+            wide = wide_s.at[t % 2]
+            wide[...] = kv[start:start + block_rows, :].astype(jnp.float32)
+            at = slice(t * half_rows, (t + 1) * half_rows)
+            keys[r // 2, at, lanes] = wide[pl.ds(0, half_rows, stride=2), :].astype(jnp.bfloat16)
+            values[r // 2, at, lanes] = wide[pl.ds(1, half_rows, stride=2), :].astype(jnp.bfloat16)
+
+    def prepare(c):
+        hc = phases[c]
+        arrived(c, starts[c], widths[c])
+        block = summed(starts[c], widths[c])
+        for h in range(hc):
+            q_s[pl.ds(h, local_rows, stride=hc), :] = rotate(
+                block[:, h * HEAD_SIZE:(h + 1) * HEAD_SIZE] * scale
+            )
+
+    for r in range(local_rows // 2):
         take(i)
         i += 1
-        lax.fori_loop(r * blocks, (r + 1) * blocks, divide, 0)
-    for c in range(last + 1):
-        wo_copy(c).start()
-
-    arrived(nc, q_width, side)
+        divide(r)
+    wo_copy(0).start()
+    arrived(last + 1, q_width, side)
     tail = summed(q_width, side)
     scale = lax.rsqrt(tail[:, kv_width:] / MODEL_WIDTH + 1e-05)
     rkey = rotate(tail[:, :HEAD_SIZE] * scale)
     value_new = tail[:, HEAD_SIZE:2 * HEAD_SIZE] * scale
+    prepare(0)
+    for r in range(local_rows // 2, local_rows):
+        take(i)
+        i += 1
+        if r == local_rows - 1:
+            for c in range(1, last + 1):
+                wo_copy(c).start()
+        divide(r)
     inv_root = np.float32(1.0 / np.sqrt(np.float32(HEAD_SIZE)))
 
     def spread(c):
@@ -245,14 +262,8 @@
 
     for c in range(last + 1):
         hc = phases[c]
-        for k in range(nc):
-            if starts[c] <= q_starts[k] < starts[c] + widths[c]:
-                arrived(k, q_starts[k], q_widths[k])
-        block = summed(starts[c], widths[c])
-        for h in range(hc):
-            q_s[pl.ds(h, local_rows, stride=hc), :] = rotate(
-                block[:, h * HEAD_SIZE:(h + 1) * HEAD_SIZE] * scale
-            )
+        if c > 0:
+            prepare(c)
         column = lax.broadcasted_iota(jnp.int32, (2 * hc, positions), 1)
         first = lax.broadcasted_iota(jnp.int32, (2 * hc, HEAD_SIZE), 0) < hc
         first_wide = lax.broadcasted_iota(jnp.int32, (2 * hc, positions), 0) < hc
@@ -423,10 +434,10 @@
         cut = [(k * size, (k + 1) * size) for k in range(parts)]
         if c == len(chunks) - 1 and size % 512 == 0:
             begin, end = cut.pop()
-            middle = (begin + end) // 2
+            middle = begin + (end - begin) * 3 // 4
             cut += [(begin, middle), (middle, end)]
         cuts.append(cut)
-    ahead = 4
+    ahead = 5
     step = min(1024, out_width)
     outs = [(start, step) for start in range(0, out_width, step)]
     freq = np.float32(ROPE_BASE) ** (
@@ -457,7 +468,7 @@
             pltpu.VMEM(interleaved.shape, bf16),
             pltpu.VMEM((total_rows, depth), bf16),
             pltpu.VMEM((total_rows, most * HEAD_SIZE), f32),
-            pltpu.VMEM((positions, HEAD_SIZE), f32),
+            pltpu.VMEM((2, positions, HEAD_SIZE), f32),
             pltpu.VMEM((local_rows // 2, positions, 2 * HEAD_SIZE), bf16),
             pltpu.VMEM((local_rows // 2, positions, 2 * HEAD_SIZE), bf16),
             pltpu.VMEM((n, local_rows, wide), f32),
@@ -470,7 +481,7 @@
             pltpu.VMEM((total_rows, out_width), f32),
             pltpu.VMEM((total_rows, out_width), bf16),
             pltpu.VMEM((3, total_rows, out_width), bf16),
-            dma((4,)), dma((ahead,)), dma, dma((len(chunks) + 1,)),
+            dma((4,)), dma((ahead,)), dma, dma((len(phases) + 1,)),
             dma, dma((len(phases),)), dma((2,)), dma((len(outs),)), dma,
         ],
         compiler_params=pltpu.CompilerParams(

time: 22.9 us -> 22.9 us (level)
  no operation moved by 1% of the time
where the time goes in v5:
time: 22.9 us; the launch traced here: 22.7 us
  Pallas kernels  22.1 us (97%)
  local copies, waits for them, and re-layouts  0.66 us (3%)
    pallas_call x1, Pallas kernels, local(): pl.pallas_call(functools.partial(kernel, n, ny, chunks, cuts, phases, ahe...  22.1 us
    unnamed x1, local copies, waits for them, and re-layouts  0.66 us

profile of v5, /device:TPU:0, one launch (start us, length us, event | category | flops | bytes accessed | tf_op | source)
XLA Modules:
  0.0 22.7 jit_solution(8698346764483910899)
XLA Ops:
  0.0 22.1 %shard_map.82 = bf16[2,8,4096]{2,1,0:T(8,128)(2,1)S(1)} custom-call(s32[2,2]{1,0:T(2,128)} %lens_hbm.1, bf16[2,8,4096]{2,1,0:T(8,128)(2,1)} %tok_hbm.1, bf16[32,128]{1,0:T(8,128)(2,1)} %bitcast.5, f32[1,128]{1,0:T(1,128)} %constant.2.clone.freq_hbm, bf16[4096,2048]{1,0:T(8,128)(2,1)} %wq_hbm.1, bf16[4096,256]{1,0:T(8,128)(2,1)} %bitcast.3, ...), custom_call_target="tpu_custom_call" | custom-call | tf_op jit(solution)/shard_map/pallas_call | solution.py:455
  22.1 0.7 %copy.10 = bf16[2,8,4096]{2,1,0:T(8,128)(2,1)} copy(bf16[2,8,4096]{2,1,0:T(8,128)(2,1)S(1)} %shard_map.82) | data formatting | bytes 262144

commit v6 on v5

--- a/solution.py
+++ b/solution.py
@@ -438,8 +438,11 @@
             cut += [(begin, middle), (middle, end)]
         cuts.append(cut)
     ahead = 5
-    step = min(1024, out_width)
-    outs = [(start, step) for start in range(0, out_width, step)]
+    blocks = (2, 3, 3)
+    eighth = out_width // 8
+    outs = [(0, out_width)]
+    if eighth % (2 * HEAD_SIZE) == 0:
+        outs = [(sum(blocks[:o]) * eighth, blocks[o] * eighth) for o in range(len(blocks))]
     freq = np.float32(ROPE_BASE) ** (
         -2.0 * np.arange(HEAD_SIZE // 2, dtype=np.float32) / HEAD_SIZE
     )

time: 22.9 us -> 22.8 us (level)
  no operation moved by 1% of the time
where the time goes in v6:
time: 22.8 us; the launch traced here: 22.7 us
  Pallas kernels  22 us (96%)
  local copies, waits for them, and re-layouts  0.66 us (3%)
    pallas_call x1, Pallas kernels, local(): pl.pallas_call(functools.partial(kernel, n, ny, chunks, cuts, phases, ahe...  22 us
    unnamed x1, local copies, waits for them, and re-layouts  0.66 us

profile of v6, /device:TPU:0, one launch (start us, length us, event | category | flops | bytes accessed | tf_op | source)
XLA Modules:
  0.0 22.7 jit_solution(8892855124077222924)
XLA Ops:
  0.0 22.0 %shard_map.82 = bf16[2,8,4096]{2,1,0:T(8,128)(2,1)S(1)} custom-call(s32[2,2]{1,0:T(2,128)} %lens_hbm.1, bf16[2,8,4096]{2,1,0:T(8,128)(2,1)} %tok_hbm.1, bf16[32,128]{1,0:T(8,128)(2,1)} %bitcast.5, f32[1,128]{1,0:T(1,128)} %constant.2.clone.freq_hbm, bf16[4096,2048]{1,0:T(8,128)(2,1)} %wq_hbm.1, bf16[4096,256]{1,0:T(8,128)(2,1)} %bitcast.3, ...), custom_call_target="tpu_custom_call" | custom-call | tf_op jit(solution)/shard_map/pallas_call | solution.py:458
  22.0 0.7 %copy.10 = bf16[2,8,4096]{2,1,0:T(8,128)(2,1)} copy(bf16[2,8,4096]{2,1,0:T(8,128)(2,1)S(1)} %shard_map.82) | data formatting | bytes 262144

commit v7 on v6

--- a/solution.py
+++ b/solution.py
@@ -437,7 +437,7 @@
             middle = begin + (end - begin) * 3 // 4
             cut += [(begin, middle), (middle, end)]
         cuts.append(cut)
-    ahead = 5
+    ahead = 6
     blocks = (2, 3, 3)
     eighth = out_width // 8
     outs = [(0, out_width)]

time: 22.8 us -> 22.8 us (level)
  no operation moved by 1% of the time
where the time goes in v7:
time: 22.8 us; the launch traced here: 22.7 us
  Pallas kernels  22 us (96%)
  local copies, waits for them, and re-layouts  0.66 us (3%)
    pallas_call x1, Pallas kernels, local(): pl.pallas_call(functools.partial(kernel, n, ny, chunks, cuts, phases, ahe...  22 us
    unnamed x1, local copies, waits for them, and re-layouts  0.66 us

profile of v7, /device:TPU:0, one launch (start us, length us, event | category | flops | bytes accessed | tf_op | source)
XLA Modules:
  0.0 22.7 jit_solution(7871897172635251965)
XLA Ops:
  0.0 22.0 %shard_map.82 = bf16[2,8,4096]{2,1,0:T(8,128)(2,1)S(1)} custom-call(s32[2,2]{1,0:T(2,128)} %lens_hbm.1, bf16[2,8,4096]{2,1,0:T(8,128)(2,1)} %tok_hbm.1, bf16[32,128]{1,0:T(8,128)(2,1)} %bitcast.5, f32[1,128]{1,0:T(1,128)} %constant.2.clone.freq_hbm, bf16[4096,2048]{1,0:T(8,128)(2,1)} %wq_hbm.1, bf16[4096,256]{1,0:T(8,128)(2,1)} %bitcast.3, ...), custom_call_target="tpu_custom_call" | custom-call | tf_op jit(solution)/shard_map/pallas_call | solution.py:458
  22.0 0.7 %copy.10 = bf16[2,8,4096]{2,1,0:T(8,128)(2,1)} copy(bf16[2,8,4096]{2,1,0:T(8,128)(2,1)S(1)} %shard_map.82) | data formatting | bytes 262144
